TPU v7x, 256 devices: a whole 4x4x8 slice. The times are simulated.
256 devices in a mesh: ctx: 16 (over x_lo, z), tp: 8 (over y, x_hi), batch: 2 (over core).
Axes of the slice: x: 4 (x_hi: 2, x_lo: 2; x = x_hi * 2 + x_lo), y: 4, z: 8, core: 2. Of those that a mesh axis runs over, the one named last changes fastest.
Arguments:
- queries: bfloat16 [4, 2048, 128, 128], P('batch', 'ctx', 'tp'), may hold values from -60 to 60, as said below
- span_key_rows: bfloat16 [4, 2048, 8, 128], P('batch', 'ctx', 'tp'), may hold values from -6 to 6
- span_value_rows: bfloat16 [4, 2048, 8, 128], P('batch', 'ctx', 'tp'), may hold values from -1.5 to 1.5
- prefix_key_rows: bfloat16 [4, 4096, 8, 128], P('batch', 'ctx', 'tp'), may hold values from -6 to 6
- prefix_value_rows: bfloat16 [4, 4096, 8, 128], P('batch', 'ctx', 'tp'), may hold values from -1.5 to 1.5
- cached_len: int32 [4], P('batch'), may hold values from 1024 to 4096
- new_len: int32 [4], P('batch'), may hold values from 1024 to 2048
- prefill_flag: int32 [4], P('batch'), may hold values from 0 to 1, as said below
- block_order: int32 [32], replicated, may hold values from 0 to 31, each once
Outputs:
- attended: bfloat16 [4, 2048, 128, 128], P('batch', 'ctx', 'tp')
Inputs may be any that keep to these rules, and one draw needn't show every extreme that they name: `queries`: large entries come in a few whole head vectors. `prefill_flag`: rows come in aligned pairs (rows 2k and 2k + 1): of each pair exactly one has the value 1.
All inputs are finite; a program needn't handle non-finite values.
Results may differ from a plain program's by a relative error of at most 0.012.
The roundings to bfloat16 on the way count: a program that leaves them out, or rounds other values in their place, can miss the bound.
Values may be sent and summed in bfloat16 or wider, within the bound.
A program may use at most 256 MiB of HBM per device.

v0:
```python
import jax
import jax.numpy as jnp
from jax import lax
from jax.sharding import PartitionSpec as P

rope_base = 500000.0
neg_large = -1e30


def sent_together(arrays, axis, dim, along):
    ends, at = ([], 0)
    for a in arrays[:-1]:
        at += a.shape[along]
        ends.append(at)
    both = jnp.concatenate(arrays, axis=along)
    return tuple(jnp.split(lax.all_gather(both, axis, axis=dim, tiled=True), ends, axis=along))


def rotate(x, positions):
    half = x.shape[-1] // 2
    inverse = rope_base ** (-(jnp.arange(half, dtype=jnp.float32) * 2.0 / x.shape[-1]))
    angle = positions.astype(jnp.float32)[:, :, None, None] * inverse
    cosine = jnp.cos(angle)
    sine = jnp.sin(angle)
    wide = x.astype(jnp.float32)
    first = wide[..., :half]
    second = wide[..., half:]
    return jnp.concatenate(
        [first * cosine - second * sine, second * cosine + first * sine], -1
    ).astype(jnp.bfloat16)


def attend(carry, q_rot, keys, values, valid):
    top, total, summed = carry
    rows, count, heads, size = q_rot.shape
    kv_heads = keys.shape[2]
    query_group = heads // kv_heads
    width = keys.shape[1]
    grouped = q_rot.reshape(rows, count, kv_heads, query_group, size)
    score = jnp.einsum("rqhgd,rnhd->rqhgn", grouped, keys, preferred_element_type=jnp.float32)
    score = score.reshape(rows, count, heads, width) * (1.0 / size**0.5)
    visible = valid[:, :, None, :]
    score = jnp.where(visible, score, neg_large)
    new_top = jnp.maximum(top, jnp.max(score, -1))
    prob = jnp.where(visible, jnp.exp(score - new_top[..., None]), 0.0)
    factor = jnp.exp(top - new_top)
    total = total * factor + jnp.sum(prob, -1)
    rounded = prob.astype(jnp.bfloat16).reshape(rows, count, kv_heads, query_group, width)
    product = jnp.einsum("rqhgn,rnhd->rqhgd", rounded, values, preferred_element_type=jnp.float32)
    summed = summed * factor[..., None] + product.reshape(rows, count, heads, size)
    return (new_top, total, summed)


def empty_carry(rows, count, heads, size):
    return (
        jnp.full((rows, count, heads), neg_large, jnp.float32),
        jnp.zeros((rows, count, heads), jnp.float32),
        jnp.zeros((rows, count, heads, size), jnp.float32),
    )


def shards(
    queries,
    span_key_rows,
    span_value_rows,
    prefix_key_rows,
    prefix_value_rows,
    cached_len,
    new_len,
    prefill_flag,
    block_order,
):
    rows, local_new, heads, size = queries.shape
    nblocks = block_order.shape[0]
    blk = local_new // 2
    ctx_place = lax.axis_index("ctx")
    block_ids = jnp.arange(nblocks, dtype=jnp.int32)

    def logical(start, count):
        stored = start + jnp.arange(count, dtype=jnp.int32)
        owner = jnp.sum(
            jnp.where((stored // blk)[:, None] == block_ids[None, :], block_order[None, :], 0), 1
        )
        return owner * blk + stored % blk

    q_index = logical(ctx_place * local_new, local_new)
    base = jnp.where(prefill_flag == 1, 0, cached_len)
    positions = base[:, None] + q_index[None, :]
    q_rot = rotate(queries, positions)
    k_rot = rotate(span_key_rows, positions)
    carry = empty_carry(rows, local_new, heads, size)
    keys, values = sent_together((k_rot, span_value_rows), "ctx", 1, 0)
    count = keys.shape[1]
    k_index = logical(jnp.int32(0), count)
    valid = (k_index[None, None, :] <= q_index[None, :, None]) & (
        k_index[None, None, :] < new_len[:, None, None]
    )
    carry = lax.cond(
        jnp.min(k_index) > jnp.max(q_index),
        lambda: carry,
        lambda: attend(carry, q_rot, keys, values, valid),
    )
    fold_keys, fold_values = sent_together((prefix_key_rows, prefix_value_rows), "ctx", 1, 0)
    count = fold_keys.shape[1]
    slot = jnp.arange(count, dtype=jnp.int32)
    live = (slot[None, :] < cached_len[:, None]) & (prefill_flag[:, None] == 0)
    fold_valid = jnp.broadcast_to(live[:, None, :], (rows, local_new, count))
    top, total, summed = attend(carry, q_rot, fold_keys, fold_values, fold_valid)
    result = summed / total[..., None]
    alive = (q_index[None, :] < new_len[:, None])[:, :, None, None]
    return jnp.where(alive, result, 0.0).astype(jnp.bfloat16)


def solution(mesh):
    return jax.shard_map(
        shards,
        mesh=mesh,
        in_specs=(
            P("batch", "ctx", "tp", None),
            P("batch", "ctx", "tp", None),
            P("batch", "ctx", "tp", None),
            P("batch", "ctx", "tp", None),
            P("batch", "ctx", "tp", None),
            P("batch"),
            P("batch"),
            P("batch"),
            P(),
        ),
        out_specs=P("batch", "ctx", "tp", None),
        check_vma=False,
    )
```

profile of v0, /device:TPU:16, one launch (start us, length us, event | category | flops | bytes accessed | tf_op | source)
XLA Modules:
  0.0 242.6 jit_solution(801169910673617518)
XLA Ops:
  6.5 0.0 all-gather.3.cloned.1.call-start
  6.6 0.7 select_reduce_fusion.3
  7.3 0.6 fusion.59
  7.9 0.8 bitcast_convert_fusion
  8.8 0.7 compare_select_fusion.2
  9.5 0.1 add_convert_fusion.1
  9.5 0.6 fusion.44
  10.1 1.6 pad_maximum_fusion.2
  11.7 0.0 all-gather.3.cloned.1.call-update
  11.7 0.0 all-gather.5.cloned.1.call-start
  11.8 1.7 pad_maximum_fusion.1
  13.5 0.0 all-gather.5.cloned.1.call-update
  13.5 0.8 select_reduce_fusion.2
  14.3 0.7 fusion.61
  16.2 0.5 multiply_cosine_fusion
  16.7 1.5 copy_convert_fusion
  18.2 0.8 subtract_convert_fusion
  19.0 0.6 pad_maximum_fusion
  19.6 0.7 broadcast_compare_fusion.3
  20.3 0.7 broadcast_compare_fusion.2
  21.0 0.7 compare_and_fusion
  21.8 64.2 %all-gather.3.cloned.1.call-done = bf16[4,2048,1,128]{3,1,0,2:T(8,128)(2,1)} async-done(((bf16[4,128,1,128]{3,1,0,2:T(8,128)(2,1)}), bf16[4,2048,1,128]{3,1,0,2:T(8,128)(2,1)}) %all-gather.3.cloned.1.call-update) | async-done | bytes 2097168 | tf_op jit(solution)/shard_map/all_gather | solution.py:16
  86.0 51.1 %conditional.1 = (f32[2,128,16]{1,2,0:T(8,128)S(1)}, f32[2,128,16]{1,2,0:T(8,128)S(1)}, f32[2,128,16,128]{1,3,2,0:T(8,128)S(1)}) conditional(s32[]{:T(128)} %convert_element_type.42, (s32[2048]{0:T(1024)S(1)}, s32[128]{0:T(128)S(1)}, s32[]{:T(128)}, s32[2]{0:T(128)}, bf16[4,2048,1,128]{3,1,0,2:T(8,128)(2,1)}, ...), branch_computations={%region_4.7_spmd, %region_7.8_spmd} | conditional | flops 4405352448 | bytes 112928808 | solution.py:98
  86.0 0.7 broadcast_compare_fusion.1
  86.7 0.3 broadcast_compare_fusion
  87.1 1.1 broadcast_and_fusion
  88.1 14.5 %fusion.4 = (f32[2,128,16]{1,2,0:T(8,128)S(1)}, f32[2,2048,128,16]{2,1,3,0:T(8,128)}) fusion(pred[2,128,2048]{1,2,0:T(8,128)(4,1)S(1)} %broadcast_and_fusion, bf16[2,128,16,128]{3,1,2,0:T(8,128)(2,1)S(1)} %get-tuple-element.120, bf16[4,2048,1,128]{3,1,0,2:T(8,128)(2,1)} %get-tuple-element.119), kind=kOutput, calls=%fused_computation.7 | convolution fusion | flops 2172645376 | bytes 36192256 | tf_op jit(solution)/shard_map/cond/branch_0_fun/rqhgd,rnhd->rqhgn/dot_general | solution.py:40
  102.7 17.4 %fusion.9 = f32[2,128,16,128]{3,1,2,0:T(8,128)} fusion(f32[2,2048,128,16]{2,1,3,0:T(8,128)} %get-tuple-element.140, f32[2,128,16]{1,2,0:T(8,128)S(1)} %get-tuple-element.149, pred[2,128,2048]{1,2,0:T(8,128)(4,1)S(1)} %broadcast_and_fusion, bf16[4,2048,1,128]{3,1,0,2:T(8,128)(2,1)} %get-tuple-element.119, f32[2,128,16]{1,2,0:T(8,128)S(1)} %get-tuple-element.131), kind=kOutput, calls=%fused_computation.11 | convolution fusion | flops 2189950976 | bytes 37257216 | tf_op jit(solution)/shard_map/cond/branch_0_fun/rqhgn,rnhd->rqhgd/dot_general | solution.py:49
  120.1 14.8 %select_reduce_fusion = f32[2,128,16]{1,2,0:T(8,128)S(1)} fusion(f32[2,2048,128,16]{2,1,3,0:T(8,128)} %get-tuple-element.140, f32[2,128,16]{1,2,0:T(8,128)S(1)} %get-tuple-element.149, pred[2,128,2048]{1,2,0:T(8,128)(4,1)S(1)} %broadcast_and_fusion), kind=kLoop, calls=%fused_computation.6 | loop fusion | flops 41938944 | bytes 34111488 | tf_op jit(solution)/shard_map/cond/branch_0_fun/reduce_sum | solution.py:47
  134.9 1.9 copy.38
  137.1 24.1 %all-gather.5.cloned.1.call-done = bf16[4,4096,1,128]{3,1,0,2:T(8,128)(2,1)} async-done(((bf16[4,256,1,128]{3,1,0,2:T(8,128)(2,1)}), bf16[4,4096,1,128]{3,1,0,2:T(8,128)(2,1)}) %all-gather.5.cloned.1.call-update) | async-done | bytes 4194320 | tf_op jit(solution)/shard_map/all_gather | solution.py:16
  161.2 25.8 %fusion.28 = (f32[2,128,16]{1,2,0:T(8,128)S(1)}, f32[2,4096,128,16]{2,1,3,0:T(8,128)}) fusion(pred[2,4096]{1,0:T(4,128)(4,1)S(1)} %compare_and_fusion, bf16[2,128,16,128]{3,1,2,0:T(8,128)(2,1)S(1)} %pad_maximum_fusion, bf16[4,4096,1,128]{3,1,0,2:T(8,128)(2,1)} %all-gather.5.cloned.1.call-done), kind=kOutput, calls=%fused_computation.39 | convolution fusion | flops 4345294848 | bytes 70279168 | tf_op jit(solution)/shard_map/rqhgd,rnhd->rqhgn/dot_general | solution.py:40
  187.0 21.5 %select_reduce_fusion.1 = f32[2,128,16]{1,2,0:T(8,128)S(1)} fusion(f32[2,4096,128,16]{2,1,3,0:T(8,128)} %get-tuple-element.148, f32[2,128,16]{1,2,0:T(8,128)S(1)} %max.3, pred[2,4096]{1,0:T(4,128)(4,1)S(1)} %compare_and_fusion), kind=kLoop, calls=%fused_computation.38 | loop fusion | flops 83881984 | bytes 67149824 | tf_op jit(solution)/shard_map/reduce_sum | solution.py:47
  208.5 25.5 %fusion.36 = bf16[2,128,16,128]{1,3,2,0:T(8,128)(2,1)S(1)} fusion(f32[2,128,16,128]{1,3,2,0:T(8,128)S(1)} %get-tuple-element.130, f32[2,4096,128,16]{2,1,3,0:T(8,128)} %get-tuple-element.148, f32[2,128,16]{1,2,0:T(8,128)S(1)} %max.3, pred[2,4096]{1,0:T(4,128)(4,1)S(1)} %compare_and_fusion, bf16[4,4096,1,128]{3,1,0,2:T(8,128)(2,1)} %all-gather.5.cloned.1.call-done, ...), kind=kOutput, calls=%fused_computation.49 | convolution fusion | flops 4381474816 | bytes 72409344 | tf_op jit(solution)/shard_map/rqhgn,rnhd->rqhgd/dot_general | solution.py:49
  234.1 1.7 copy.29
  (9 shorter events, 0.1 us)
Async XLA Ops:
  6.5 79.4 %all-gather.3.cloned.1.call-start = ((), (), s32[]{:S(2)}) async-start(), calls=%async_computation | async-start | bytes 2228224 | tf_op jit(solution)/shard_map/all_gather | solution.py:16
  11.7 149.5 %all-gather.5.cloned.1.call-start = ((), (), s32[]{:S(2)}) async-start(), calls=%async_computation.1 | async-start | bytes 4456448 | tf_op jit(solution)/shard_map/all_gather | solution.py:16
Sparse Core Ops, SparseCore 0:
  11.8 74.0 all-gather.2
  87.7 73.3 all-gather.4
where the time goes:
time: 243 us
  waiting for transfers between devices  88.3 us (36%)
  matrix products  83.3 us (34%)
  other arithmetic  52.3 us (22%)
  between operations  14.7 us (6%)
  local copies, waits for them, and re-layouts  3.61 us (1%)
    all_gather x2, waiting for transfers between devices, sent_together(): lax.all_gather(both, axis, axis=dim, tiled=True)  88.3 us
    dot_general x2, matrix products, attend(): jnp.einsum('rqhgn,rnhd->rqhgd', rounded, values, preferred_element_type=j...  42.9 us
    dot_general x2, matrix products, attend(): jnp.einsum('rqhgd,rnhd->rqhgn', grouped, keys, preferred_element_type=jnp...  40.4 us
    reduce_sum x2, other arithmetic, attend(): total = total * factor + jnp.sum(prob, -1)  36.3 us
  transfers between devices with their start and end apart: 2, of which 2 were waited for; matrix products, arithmetic and copies ran while one was open for 25% of the time, Pallas kernels for 0%

commit v1 on v0

v1 whole, which is shorter than its diff:
```python
import functools
import math

import jax
import jax.numpy as jnp
from jax import lax
from jax.experimental import pallas as pl
from jax.experimental.pallas import tpu as pltpu
from jax.sharding import PartitionSpec as P

ROPE_BASE = 500000.0
NEG = -1e30
TILE = 256
MESH = pl.DeviceIdType.MESH


def trig_tables(positions, size):
    half = size // 2
    inverse = ROPE_BASE ** (-(jnp.arange(half, dtype=jnp.float32) * 2.0 / size))
    angle = positions.astype(jnp.float32)[:, :, None] * inverse
    cosine, sine = jnp.cos(angle), jnp.sin(angle)
    return jnp.concatenate([cosine, cosine], -1), jnp.concatenate([-sine, sine], -1)


def prep_kernel(flag, cos, sin, sk, sv, ck, cv, f_out, g_out):
    half = sk.shape[-1] // 2
    a = flag[0]
    for piece, row in enumerate((a, 1 - a)):
        x = sk[row].astype(jnp.float32)
        turned = x * cos[row] + pltpu.roll(x, half, 1) * sin[row]
        f_out[piece] = turned.astype(jnp.bfloat16)
        f_out[2 + piece] = sv[row].astype(jnp.float32).T.astype(jnp.bfloat16)
    n = ck.shape[1] // 2
    for part in range(2):
        g_out[part] = ck[a, part * n : (part + 1) * n]
        g_out[2 + part] = cv[a, part * n : (part + 1) * n].astype(jnp.float32).T.astype(jnp.bfloat16)


def main_kernel(
    nz, flag, clen, nlen, order, q, cos, sin, fown, gown, out,
    fbuf, gbuf, qt, kx, vx, s0, s1, acc, top, tot,
    f_send, f_recv, g_send, g_recv, gz_send, gz_recv,
):
    me = lax.axis_index("ctx")
    column, z = me // nz, me % nz
    other = (1 - column) * nz + z

    def mine(d):
        return column * nz + (z + d + nz) % nz

    def theirs(d):
        return (1 - column) * nz + (z + d + nz) % nz

    up, down = mine(1), mine(-1)

    barrier = pltpu.get_barrier_semaphore()
    for peer in (up, down, other):
        pl.semaphore_signal(barrier, inc=1, device_id={"ctx": peer}, device_id_type=MESH)
    pl.semaphore_wait(barrier, 3)

    started = []
    counts = {"f": 0, "g": 0, "z": 0}
    sends = {"f": f_send, "g": g_send, "z": gz_send}
    recvs = {"f": f_recv, "g": g_recv, "z": gz_recv}

    def send(kind, src, dst, slot, peer):
        c = pltpu.make_async_remote_copy(
            src_ref=src, dst_ref=dst, send_sem=sends[kind].at[counts[kind]], recv_sem=recvs[kind].at[slot],
            device_id={"ctx": peer}, device_id_type=MESH,
        )
        counts[kind] += 1
        c.start()
        started.append(c)

    def send_f(slot, peer, own=False):
        send("f", fown if own else fbuf.at[slot], fbuf.at[slot], slot, peer)

    def send_g(slot, peer, own=False):
        send("g", gown if own else gbuf.at[slot], gbuf.at[slot], slot, peer)

    def send_half(slot, part, peer):
        ref = gbuf.at[slot, pl.ds(2 * part, 2)]
        send("z", ref, ref, part, peer)

    def got(buf, sem):
        pltpu.make_async_remote_copy(
            src_ref=buf, dst_ref=buf, send_sem=f_send.at[0], recv_sem=sem, device_id={"ctx": other}, device_id_type=MESH
        ).wait_recv()

    def got_f(slot):
        got(fbuf.at[slot], f_recv.at[slot])

    def got_g(slot):
        got(gbuf.at[slot], g_recv.at[slot])

    send_g(me, up, True)
    send_g(me, down, True)
    send_f(me, other, True)
    send_f(me, up, True)
    send_f(me, down, True)
    send_g(me, other, True)

    rows, count, heads, size = q.shape
    half = size // 2
    group = TILE // heads
    tiles = count // group
    swap = flag[0] == 1
    scale = math.log2(math.e) / math.sqrt(size)

    def prepare(t, _):
        here = pl.ds(pl.multiple_of(t * group, group), group)
        turned = []
        for r in range(rows):
            x = q[r, here].astype(jnp.float32)
            c, s = cos[r, here], sin[r, here]
            y = x * c[:, None, :] + pltpu.roll(x, half, 2) * s[:, None, :]
            turned.append(y.reshape(TILE, size))
        place = t * group + lax.broadcasted_iota(jnp.int32, (size, TILE), 1) // heads
        hot = jnp.where(lax.broadcasted_iota(jnp.int32, (size, TILE), 0) == place, 1.0, 0.0).astype(jnp.bfloat16)
        for r, y in enumerate((jnp.where(swap, turned[1], turned[0]), jnp.where(swap, turned[0], turned[1]))):
            at = r * tiles + t
            qt[at, 0:size] = y.T.astype(jnp.bfloat16)
            qt[at, size : 2 * size] = hot
            acc[at] = jnp.zeros((size, TILE), jnp.float32)
            top[at] = jnp.full((1, TILE), NEG, jnp.float32)
            tot[at] = jnp.zeros((1, TILE), jnp.float32)
        return 0

    lax.fori_loop(0, tiles, prepare, 0)

    piece = fown.shape[1]
    cached = jnp.where(swap, clen[1], clen[0])
    live = (jnp.where(swap, nlen[1], nlen[0]), jnp.where(swap, nlen[0], nlen[1]))
    blk = piece // 2
    lane = lax.broadcasted_iota(jnp.int32, (piece, size), 1)
    line = lax.broadcasted_iota(jnp.int32, (piece, size), 0)

    def logical(slot, i):
        first, second = order[2 * slot], order[2 * slot + 1]
        return jnp.where(i < blk, first * blk + i, second * blk + i - blk)

    q_index = logical(me, lane)

    def bias(visible):
        return jnp.where(visible, 0.0, NEG).astype(jnp.bfloat16)

    def scores(at, row):
        return jnp.dot(kx[row], qt[at], preferred_element_type=jnp.float32)

    def absorb(s_ref, at, row):
        s = s_ref[...]
        old = top[at]
        new = jnp.maximum(old, jnp.max(s, axis=0, keepdims=True))
        p = jnp.exp2((s - new) * scale)
        fade = jnp.exp2((old - new) * scale)
        tot[at] = tot[at] * fade + jnp.sum(p, axis=0, keepdims=True)
        acc[at] = acc[at] * fade + jnp.dot(vx[row], p.astype(jnp.bfloat16), preferred_element_type=jnp.float32)
        top[at] = new

    def compute(total):
        s0[...] = scores(0, 0)

        def step(u, _):
            t0 = 2 * u
            t1, t2 = t0 + 1, jnp.minimum(t0 + 2, total - 1)
            s1[...] = scores(t1, t1 // tiles)
            absorb(s0, t0, t0 // tiles)
            s0[...] = scores(t2, t2 // tiles)
            absorb(s1, t1, t1 // tiles)
            return 0

        lax.fori_loop(0, total // 2, step, 0)

    def cache_chunk(*blocks):
        for j, (ref, slot) in enumerate(blocks):
            for h in range(2):
                at = (2 * j + h) * piece
                kx[0, at : at + piece, 0:size] = ref[h]
                kx[0, at : at + piece, size : 2 * size] = bias(slot * 2 * piece + h * piece + line < cached)
                vx[0, :, at : at + piece] = ref[2 + h]
        compute(tiles)

    def span_chunk(*blocks):
        for j, (ref, slot) in enumerate(blocks):
            at = j * piece
            k_index = logical(slot, line)
            for r in range(2):
                kx[r, at : at + piece, 0:size] = ref[r]
                kx[r, at : at + piece, size : 2 * size] = bias((k_index <= q_index) & (k_index < live[r]))
                vx[r, :, at : at + piece] = ref[2 + r]
        compute(2 * tiles)

    def gb(slot):
        return gbuf.at[slot], slot

    def fb(slot):
        return fbuf.at[slot], slot

    last = nz // 2

    got_f(other)
    send_f(other, up)
    send_f(other, down)
    for d in (1, -1):
        got_g(mine(d))
        send_g(mine(d), down if d > 0 else up)
        send_g(mine(d), other)
    cache_chunk(gb(mine(1)), gb(mine(-1)))
    for d in (1, -1):
        got_f(mine(d))
        send_f(mine(d), down if d > 0 else up)
    got_g(other)
    cache_chunk((gown, me), gb(other))
    for d in (1, -1):
        got_f(theirs(d))
        send_f(theirs(d), down if d > 0 else up)
    for d in (2, -2):
        got_g(mine(d))
        send_g(mine(d), down if d > 0 else up)
        send_g(mine(d), other)
    span_chunk((fown, me), fb(other), fb(mine(1)), fb(mine(-1)))
    for d in (2, -2):
        got_f(mine(d))
        send_f(mine(d), down if d > 0 else up)
    got_g(theirs(1))
    got_g(theirs(-1))
    cache_chunk(gb(theirs(1)), gb(theirs(-1)))
    for d in (2, -2):
        got_f(theirs(d))
        send_f(theirs(d), down if d > 0 else up)
    for d in (3, -3):
        got_g(mine(d))
        send_half(mine(d), 0 if d < 0 else 1, up if d < 0 else down)
        send_g(mine(d), other)
    cache_chunk(gb(mine(2)), gb(mine(-2)))
    far = mine(last)
    for part in range(2):
        got(gbuf.at[far, pl.ds(2 * part, 2)], gz_recv.at[part])
    send_g(far, other)
    span_chunk(fb(theirs(1)), fb(theirs(-1)), fb(mine(2)), fb(mine(-2)))
    got_f(mine(3))
    got_f(mine(-3))
    send_f(mine(-3), up)
    got_g(theirs(2))
    got_g(theirs(-2))
    cache_chunk(gb(theirs(2)), gb(theirs(-2)))
    got_f(theirs(3))
    got_f(theirs(-3))
    send_f(theirs(3), down)
    cache_chunk(gb(mine(3)), gb(mine(-3)))
    span_chunk(fb(theirs(2)), fb(theirs(-2)), fb(mine(3)), fb(mine(-3)))
    got_g(theirs(3))
    got_g(theirs(-3))
    cache_chunk(gb(theirs(3)), gb(theirs(-3)))
    got_g(theirs(last))
    cache_chunk(gb(far), gb(theirs(last)))
    got_f(far)
    got_f(theirs(last))
    span_chunk(fb(theirs(3)), fb(theirs(-3)), fb(far), fb(theirs(last)))

    def finish(t, _):
        here = pl.ds(pl.multiple_of(t * group, group), group)
        done = [(acc[r * tiles + t] / tot[r * tiles + t]).T.reshape(group, heads, size) for r in range(2)]
        i = logical(me, t * group + lax.broadcasted_iota(jnp.int32, (group, heads, size), 0))
        for r in range(2):
            value = jnp.where(swap, done[1 - r], done[r])
            out[r, here] = jnp.where(i < nlen[r], value, 0.0).astype(out.dtype)
        return 0

    lax.fori_loop(0, tiles, finish, 0)
    for c in started:
        c.wait_send()


def shards(nz, queries, span_k, span_v, cache_k, cache_v, cached_len, new_len, prefill_flag, block_order):
    rows, count, heads, size = queries.shape
    n_ctx = lax.axis_size("ctx")
    nblocks = block_order.shape[0]
    blk = count * n_ctx // nblocks
    me = lax.axis_index("ctx")
    index = (lax.dynamic_slice(block_order, (2 * me,), (2,))[:, None] * blk + jnp.arange(blk, dtype=jnp.int32)).reshape(count)
    base = jnp.where(prefill_flag == 1, 0, cached_len)
    cos, sin = trig_tables(base[:, None] + index[None, :], size)

    smem = pl.BlockSpec(memory_space=pltpu.SMEM)
    vmem = pl.BlockSpec(memory_space=pltpu.VMEM)
    packed = jax.ShapeDtypeStruct((4, count, size), jnp.bfloat16)
    fown, gown = pl.pallas_call(
        prep_kernel,
        out_shape=(packed, packed),
        in_specs=[smem] + [vmem] * 6,
        out_specs=(vmem, vmem),
        name="prep",
    )(prefill_flag, cos, sin, span_k[:, :, 0], span_v[:, :, 0], cache_k[:, :, 0], cache_v[:, :, 0])

    tiles = count * heads // TILE
    keys = 4 * count
    bf16, f32, dma = jnp.bfloat16, jnp.float32, pltpu.SemaphoreType.DMA
    return pl.pallas_call(
        functools.partial(main_kernel, nz),
        out_shape=jax.ShapeDtypeStruct(queries.shape, queries.dtype),
        in_specs=[smem] * 4 + [vmem] * 5,
        out_specs=vmem,
        scratch_shapes=[
            pltpu.VMEM((n_ctx, 4, count, size), bf16),
            pltpu.VMEM((n_ctx, 4, count, size), bf16),
            pltpu.VMEM((2 * tiles, 2 * size, TILE), bf16),
            pltpu.VMEM((2, keys, 2 * size), bf16),
            pltpu.VMEM((2, size, keys), bf16),
            pltpu.VMEM((keys, TILE), f32),
            pltpu.VMEM((keys, TILE), f32),
            pltpu.VMEM((2 * tiles, size, TILE), f32),
            pltpu.VMEM((2 * tiles, 1, TILE), f32),
            pltpu.VMEM((2 * tiles, 1, TILE), f32),
            dma((2 * n_ctx,)),
            dma((n_ctx,)),
            dma((2 * n_ctx,)),
            dma((n_ctx,)),
            dma((2,)),
            dma((2,)),
        ],
        compiler_params=pltpu.CompilerParams(collective_id=0, has_side_effects=True, vmem_limit_bytes=48 * 1024 * 1024),
        name="gather_attend",
    )(prefill_flag, cached_len, new_len, block_order, queries, cos, sin, fown, gown)


def solution(mesh):
    nz = mesh.shape["ctx"] // 2
    four = P("batch", "ctx", "tp", None)
    return jax.shard_map(
        functools.partial(shards, nz),
        mesh=mesh,
        in_specs=(four,) * 5 + (P("batch"),) * 3 + (P(),),
        out_specs=four,
        check_vma=False,
    )
```

time: 243 us -> 70.1 us (0.29)
  waiting for transfers between devices: 88.3 us -> 0 us
  matrix products: 83.3 us -> 0 us
  Pallas kernels: 0 us -> 63.4 us
  other arithmetic: 52.3 us -> 3.01 us
  between operations: 14.7 us -> 0.06 us
    all_gather x2 -> x0, waiting for transfers between devices: 88.3 us -> none  [sent_together(): lax.all_gather(both, axis, axis=dim, tiled=True)]
    dot_general x4 -> x0, matrix products: 83.3 us -> none  [the longest x2 42.9 us: attend(): jnp.einsum('rqhgn,rnhd->rqhgd', rounded, values, preferred_element_type=j...]
    pallas_call x0 -> x2, Pallas kernels: none -> 63.4 us  [the longest x1 61.3 us: shards(): pl.pallas_call(functools.partial(main_kernel, nz), out_shape=jax.ShapeDty...]
    reduce_sum x4 -> x0, other arithmetic: 37.8 us -> none  [the longest x2 36.3 us: attend(): total = total * factor + jnp.sum(prob, -1)]
    unnamed x0 -> x19, local copies, waits for them, and re-layouts: none -> 3.43 us
    concatenate x3 -> x1, other arithmetic: 3.85 us -> 0.82 us  [trig_tables(): jnp.concatenate([cosine, cosine], -1)]
  transfers between devices with their start and end apart: 2 -> 0, of which waited for: 2 -> 0; matrix products, arithmetic and copies ran while one was open for 25% -> 0% of each run, Pallas kernels for 0% -> 0%
where the time goes in v1:
time: 70.1 us; the launch traced here: 70 us
  Pallas kernels  63.4 us (90%)
  local copies, waits for them, and re-layouts  3.52 us (5%)
  other arithmetic  3.01 us (4%)
    pallas_call x1, Pallas kernels, shards(): pl.pallas_call(functools.partial(main_kernel, nz), out_shape=jax.ShapeDty...  61.3 us
    unnamed x19, local copies, waits for them, and re-layouts  3.43 us
    pallas_call x1, Pallas kernels, shards(): pl.pallas_call(prep_kernel, out_shape=(packed, packed), in_specs=[smem] +...  2.04 us

profile of v1, /device:TPU:16, one launch (start us, length us, event | category | flops | bytes accessed | tf_op | source)
XLA Modules:
  0.0 70.0 jit_solution(6181431732521999154)
XLA Ops:
  0.0 0.0 copy-start.2
  0.0 0.8 %dynamic-slice_multiply_fusion = s32[2]{0:T(128)S(1)} fusion(s32[32]{0:T(128)} %order.1, s32[]{:T(128)S(6)} %select_n.8), kind=kLoop, calls=%fused_computation.9 | loop fusion | flops 2 | bytes 20 | tf_op jit(solution)/shard_map/mul | solution.py:281
  0.8 0.1 iota_add_fusion
  0.9 0.1 add.45
  1.0 0.7 compare_select_fusion
  1.7 0.1 add_convert_fusion
  1.7 0.5 fusion
  2.3 0.8 %pad_maximum_fusion = (f32[2,128,128]{2,1,0:T(8,128)}, f32[2,128,128]{2,1,0:T(8,128)}) fusion(f32[2,128,64]{2,1,0:T(8,128)S(1)} %get-tuple-element.11, f32[2,128,64]{2,1,0:T(8,128)S(1)} %get-tuple-element.10, f32[2,128,64]{2,1,0:T(8,128)S(1)} %get-tuple-element.9), kind=kLoop, calls=%fused_computation.2 | loop fusion | flops 65536 | bytes 458752 | tf_op jit(solution)/shard_map/concatenate | solution.py:22
  3.1 0.0 copy-start
  3.1 0.0 copy-start.1
  3.1 0.0 copy-start.8
  3.1 2.0 %prep.1 = (bf16[4,128,128]{2,1,0:T(8,128)(2,1)}, bf16[4,128,128]{2,1,0:T(8,128)(2,1)}) custom-call(s32[2]{0:T(128)} %flag.3, f32[2,128,128]{2,1,0:T(8,128)} %get-tuple-element.12.cos, f32[2,128,128]{2,1,0:T(8,128)} %get-tuple-element.13.sin, bf16[2,128,128]{2,1,0:T(8,128)(2,1)} %bitcast.6, bf16[2,128,128]{2,1,0:T(8,128)(2,1)} %bitcast.7, ...), custom_call_target="tpu_custom_call" | custom-call | tf_op jit(solution)/shard_map/prep/pallas_call | solution.py:288
  5.1 0.0 copy-start.5
  5.1 0.0 copy-start.6
  5.2 0.0 copy-start.7
  5.2 0.0 copy-done.2
  5.2 0.0 copy-done
  5.2 0.0 copy-done.1
  5.2 0.0 copy-done.8
  5.2 0.6 copy-done.5
  5.8 0.0 copy-done.6
  5.8 0.0 copy-done.7
  5.8 0.0 copy-start.3
  5.8 0.9 %copy-done.3 = bf16[4,128,128]{2,1,0:T(8,128)(2,1)S(1)} copy-done((bf16[4,128,128]{2,1,0:T(8,128)(2,1)S(1)}, bf16[4,128,128]{2,1,0:T(8,128)(2,1)}, u32[]{:S(2)}) %copy-start.3) | copy-done | bytes 131096
  6.7 0.0 copy-start.4
  6.7 0.9 %copy-done.4 = bf16[4,128,128]{2,1,0:T(8,128)(2,1)S(1)} copy-done((bf16[4,128,128]{2,1,0:T(8,128)(2,1)S(1)}, bf16[4,128,128]{2,1,0:T(8,128)(2,1)}, u32[]{:S(2)}) %copy-start.4) | copy-done | bytes 131096
  7.6 61.3 %gather_attend.1 = bf16[2,128,16,128]{3,2,1,0:T(8,128)(2,1)S(1)} custom-call(s32[2]{0:T(128)S(1)} %copy-done.5, s32[2]{0:T(128)S(1)} %copy-done.6, s32[2]{0:T(128)S(1)} %copy-done.7, s32[32]{0:T(128)S(1)} %copy-done.8, bf16[2,128,16,128]{3,2,1,0:T(8,128)(2,1)S(1)} %copy-done.2, f32[2,128,128]{2,1,0:T(8,128)S(1)} %copy-done, f32[2,128,128]{2,1,0:T(8,128)S(1)} %copy-done.1, ...), custom_call_target="tpu_custom_call" | custom-call | tf_op jit(solution)/shard_map/gather_attend/pallas_call | solution.py:299
  69.0 1.0 %copy.11 = bf16[2,128,16,128]{3,2,1,0:T(8,128)(2,1)} copy(bf16[2,128,16,128]{3,2,1,0:T(8,128)(2,1)S(1)} %gather_attend.1) | data formatting | bytes 2097152
  (1 shorter events, 0.0 us)
Async XLA Ops:
  0.0 5.2 %copy-start.2 = (bf16[2,128,16,128]{3,2,1,0:T(8,128)(2,1)S(1)}, bf16[2,128,16,128]{3,2,1,0:T(8,128)(2,1)}, u32[]{:S(2)}) copy-start(bf16[2,128,16,128]{3,2,1,0:T(8,128)(2,1)} %q.1) | copy-start | bytes 3145732
  3.1 2.1 %copy-start = (f32[2,128,128]{2,1,0:T(8,128)S(1)}, f32[2,128,128]{2,1,0:T(8,128)}, u32[]{:S(2)}) copy-start(f32[2,128,128]{2,1,0:T(8,128)} %get-tuple-element.12.cos) | copy-start | bytes 393220
  3.1 2.1 %copy-start.1 = (f32[2,128,128]{2,1,0:T(8,128)S(1)}, f32[2,128,128]{2,1,0:T(8,128)}, u32[]{:S(2)}) copy-start(f32[2,128,128]{2,1,0:T(8,128)} %get-tuple-element.13.sin) | copy-start | bytes 393220
  3.1 2.1 %copy-start.8 = (s32[32]{0:T(128)S(1)}, s32[32]{0:T(128)}, u32[]{:S(2)}) copy-start(s32[32]{0:T(128)} %order.1) | copy-start | bytes 388
  5.1 0.7 copy-start.5
  5.1 0.7 copy-start.6
  5.2 0.7 copy-start.7
  5.8 0.9 %copy-start.3 = (bf16[4,128,128]{2,1,0:T(8,128)(2,1)S(1)}, bf16[4,128,128]{2,1,0:T(8,128)(2,1)}, u32[]{:S(2)}) copy-start(bf16[4,128,128]{2,1,0:T(8,128)(2,1)} %get-tuple-element.7.fown) | copy-start | bytes 393220
  6.7 0.9 %copy-start.4 = (bf16[4,128,128]{2,1,0:T(8,128)(2,1)S(1)}, bf16[4,128,128]{2,1,0:T(8,128)(2,1)}, u32[]{:S(2)}) copy-start(bf16[4,128,128]{2,1,0:T(8,128)(2,1)} %get-tuple-element.8.gown) | copy-start | bytes 393220

commit v2 on v1

v2 whole, which is shorter than its diff:
```python
import functools
import math

import jax
import jax.numpy as jnp
from jax import lax
from jax.experimental import pallas as pl
from jax.experimental.pallas import tpu as pltpu
from jax.sharding import PartitionSpec as P

ROPE_BASE = 500000.0
NEG = -1e30
TILE = 256
MESH = pl.DeviceIdType.MESH


HALF_PI = (1.5703125, 4.837512969970703125e-4, 7.54978995489188216e-8)


def turn_tables(positions, inverse, sign):
    angle = positions * inverse
    quarter = jnp.floor(angle * (2.0 / math.pi) + 0.5)
    x = ((angle - quarter * HALF_PI[0]) - quarter * HALF_PI[1]) - quarter * HALF_PI[2]
    z = x * x
    sine = ((-1.9515295891e-4 * z + 8.3321608736e-3) * z - 1.6666654611e-1) * z * x + x
    cosine = ((2.443315711809948e-5 * z - 1.388731625493765e-3) * z + 4.166664568298827e-2) * z * z - 0.5 * z + 1.0
    n = quarter.astype(jnp.int32)
    odd = (n & 1) == 1
    c = jnp.where(odd, sine, cosine)
    s = jnp.where(odd, cosine, sine)
    c = jnp.where(((n + 1) & 2) == 2, -c, c)
    s = jnp.where((n & 2) == 2, -s, s)
    return c, s * sign


def main_kernel(
    nz, flag, clen, nlen, order, q_hbm, sk_hbm, sv_hbm, ck_hbm, cv_hbm, out,
    q, sk, sv, ck, cv, cos, sin, fbuf, gbuf, qt, kx, vx, s_tiles, m_tiles, acc, top, tot,
    in_sem, f_send, f_recv, g_send, g_recv, gz_send, gz_recv,
):
    loads = [
        pltpu.make_async_copy(src, dst, in_sem.at[i])
        for i, (src, dst) in enumerate(((ck_hbm, ck), (cv_hbm, cv), (sk_hbm, sk), (sv_hbm, sv), (q_hbm, q)))
    ]
    for c in loads:
        c.start()
    me = lax.axis_index("ctx")
    column, z = me // nz, me % nz
    other = (1 - column) * nz + z

    def mine(d):
        return column * nz + (z + d + nz) % nz

    def theirs(d):
        return (1 - column) * nz + (z + d + nz) % nz

    up, down = mine(1), mine(-1)

    barrier = pltpu.get_barrier_semaphore()
    for peer in (up, down, other):
        pl.semaphore_signal(barrier, inc=1, device_id={"ctx": peer}, device_id_type=MESH)

    rows, count, heads, size = q.shape
    half = size // 2
    group = TILE // heads
    tiles = count // group
    piece = fbuf.shape[2]
    blk = piece // 2
    swap = flag[0] == 1
    scale = math.log2(math.e) / math.sqrt(size)
    cached = jnp.where(swap, clen[1], clen[0])
    live = (jnp.where(swap, nlen[1], nlen[0]), jnp.where(swap, nlen[0], nlen[1]))
    lane = lax.broadcasted_iota(jnp.int32, (piece, size), 1)
    line = lax.broadcasted_iota(jnp.int32, (piece, size), 0)

    def logical(slot, i):
        first, second = order[2 * slot], order[2 * slot + 1]
        return jnp.where(i < blk, first * blk + i, second * blk + i - blk)

    def pick(ref, r, at=slice(None)):
        return jnp.where(swap, ref[1 - r, at].astype(jnp.float32), ref[r, at].astype(jnp.float32))

    loads[0].wait()
    loads[1].wait()
    for h in range(2):
        at = slice(h * piece, (h + 1) * piece)
        gbuf[me, h] = pick(ck, 0, at).astype(jnp.bfloat16)
        gbuf[me, 2 + h] = pick(cv, 0, at).T.astype(jnp.bfloat16)
    loads[2].wait()
    loads[3].wait()
    k = (lane % half).astype(jnp.float32)
    inverse = jnp.exp2(k * (-2.0 / size * math.log2(ROPE_BASE)))
    sign = jnp.where(lane < half, -1.0, 1.0)
    index = logical(me, line)
    for r, base in enumerate((cached, 0)):
        cos[r], sin[r] = turn_tables((index + base).astype(jnp.float32), inverse, sign)
        x = pick(sk, r)
        fbuf[me, r] = (x * cos[r] + pltpu.roll(x, half, 1) * sin[r]).astype(jnp.bfloat16)
        fbuf[me, 2 + r] = pick(sv, r).T.astype(jnp.bfloat16)

    pl.semaphore_wait(barrier, 3)
    started = []
    counts = {"f": 0, "g": 0, "z": 0}
    sends = {"f": f_send, "g": g_send, "z": gz_send}
    recvs = {"f": f_recv, "g": g_recv, "z": gz_recv}

    def send(kind, src, dst, slot, peer):
        c = pltpu.make_async_remote_copy(
            src_ref=src, dst_ref=dst, send_sem=sends[kind].at[counts[kind]], recv_sem=recvs[kind].at[slot],
            device_id={"ctx": peer}, device_id_type=MESH,
        )
        counts[kind] += 1
        c.start()
        started.append(c)

    def send_f(slot, peer):
        send("f", fbuf.at[slot], fbuf.at[slot], slot, peer)

    def send_g(slot, peer):
        send("g", gbuf.at[slot], gbuf.at[slot], slot, peer)

    def send_half(slot, part, peer):
        ref = gbuf.at[slot, pl.ds(2 * part, 2)]
        send("z", ref, ref, part, peer)

    def got(buf, sem):
        pltpu.make_async_remote_copy(
            src_ref=buf, dst_ref=buf, send_sem=f_send.at[0], recv_sem=sem, device_id={"ctx": other}, device_id_type=MESH
        ).wait_recv()

    def got_f(slot):
        got(fbuf.at[slot], f_recv.at[slot])

    def got_g(slot):
        got(gbuf.at[slot], g_recv.at[slot])

    send_g(me, up)
    send_g(me, down)
    send_f(me, other)
    send_f(me, up)
    send_f(me, down)
    send_g(me, other)

    loads[4].wait()

    def prepare(t, _):
        here = pl.ds(pl.multiple_of(t * group, group), group)
        place = t * group + lax.broadcasted_iota(jnp.int32, (size, TILE), 1) // heads
        hot = jnp.where(lax.broadcasted_iota(jnp.int32, (size, TILE), 0) == place, 1.0, 0.0).astype(jnp.bfloat16)
        for r in range(rows):
            at = r * tiles + t
            x = pick(q, r, here)
            y = x * cos[r, here][:, None, :] + pltpu.roll(x, half, 2) * sin[r, here][:, None, :]
            qt[at, 0:size] = y.reshape(TILE, size).T.astype(jnp.bfloat16)
            qt[at, size : 2 * size] = hot
            acc[at] = jnp.zeros((size, TILE), jnp.float32)
            top[at] = jnp.full((1, TILE), NEG, jnp.float32)
            tot[at] = jnp.zeros((1, TILE), jnp.float32)
        return 0

    lax.fori_loop(0, tiles, prepare, 0)

    q_index = logical(me, lane)

    def bias(visible):
        return jnp.where(visible, 0.0, NEG).astype(jnp.bfloat16)

    def scores(t, at, row):
        s = jnp.dot(kx[row], qt[at], preferred_element_type=jnp.float32)
        s_tiles[t][...] = s
        m_tiles[t][...] = jnp.max(s, axis=0, keepdims=True)

    def absorb(t, at, row):
        old = top[at]
        new = jnp.maximum(old, m_tiles[t][...])
        p = jnp.exp2((s_tiles[t][...] - new) * scale)
        fade = jnp.exp2((old - new) * scale)
        tot[at] = tot[at] * fade + jnp.sum(p, axis=0, keepdims=True)
        acc[at] = acc[at] * fade + jnp.dot(vx[row], p.astype(jnp.bfloat16), preferred_element_type=jnp.float32)
        top[at] = new

    def compute(row):
        ahead = 2
        for t in range(ahead):
            scores(t, row * tiles + t, row)
        for t in range(tiles):
            if t + ahead < tiles:
                scores(t + ahead, row * tiles + t + ahead, row)
            absorb(t, row * tiles + t, row)

    def cache_chunk(*blocks):
        for j, (ref, slot) in enumerate(blocks):
            for h in range(2):
                at = (2 * j + h) * piece
                kx[0, at : at + piece, 0:size] = ref[h]
                kx[0, at : at + piece, size : 2 * size] = bias(slot * 2 * piece + h * piece + line < cached)
                vx[0, :, at : at + piece] = ref[2 + h]
        compute(0)

    def span_chunk(*blocks):
        for j, (ref, slot) in enumerate(blocks):
            at = j * piece
            k_index = logical(slot, line)
            for r in range(2):
                kx[r, at : at + piece, 0:size] = ref[r]
                kx[r, at : at + piece, size : 2 * size] = bias((k_index <= q_index) & (k_index < live[r]))
                vx[r, :, at : at + piece] = ref[2 + r]

        def one(r, _):
            compute(r)
            return 0

        lax.fori_loop(0, 2, one, 0)

    def gb(slot):
        return gbuf.at[slot], slot

    def fb(slot):
        return fbuf.at[slot], slot

    last = nz // 2

    def on(d):
        return down if d > 0 else up

    def pass_f(*slots):
        for slot, d in slots:
            got_f(slot)
            send_f(slot, on(d))

    def pass_g(*distances):
        for d in distances:
            got_g(mine(d))
            send_g(mine(d), on(d))
            send_g(mine(d), other)

    got_f(other)
    send_f(other, up)
    send_f(other, down)
    pass_g(1, -1)
    cache_chunk(gb(mine(1)), gb(mine(-1)))
    pass_f((mine(1), 1), (mine(-1), -1))
    got_g(other)
    cache_chunk(gb(me), gb(other))
    span_chunk(fb(me), fb(other), fb(mine(1)), fb(mine(-1)))
    pass_f((theirs(1), 1), (theirs(-1), -1))
    pass_g(2, -2)
    got_g(theirs(1))
    got_g(theirs(-1))
    cache_chunk(gb(theirs(1)), gb(theirs(-1)))
    cache_chunk(gb(mine(2)), gb(mine(-2)))
    pass_f((mine(2), 2), (mine(-2), -2))
    span_chunk(fb(theirs(1)), fb(theirs(-1)), fb(mine(2)), fb(mine(-2)))
    pass_f((theirs(2), 2), (theirs(-2), -2))
    for d in (3, -3):
        got_g(mine(d))
        send_half(mine(d), 0 if d < 0 else 1, on(d))
        send_g(mine(d), other)
    got_g(theirs(2))
    got_g(theirs(-2))
    cache_chunk(gb(theirs(2)), gb(theirs(-2)))
    cache_chunk(gb(mine(3)), gb(mine(-3)))
    got_f(mine(3))
    got_f(mine(-3))
    send_f(mine(-3), up)
    span_chunk(fb(theirs(2)), fb(theirs(-2)), fb(mine(3)), fb(mine(-3)))
    got_f(theirs(3))
    got_f(theirs(-3))
    send_f(theirs(3), down)
    far = mine(nz // 2)
    for part in range(2):
        got(gbuf.at[far, pl.ds(2 * part, 2)], gz_recv.at[part])
    send_g(far, other)
    got_g(theirs(3))
    got_g(theirs(-3))
    cache_chunk(gb(theirs(3)), gb(theirs(-3)))
    got_f(far)
    got_f(theirs(nz // 2))
    span_chunk(fb(theirs(3)), fb(theirs(-3)), fb(far), fb(theirs(nz // 2)))
    got_g(theirs(nz // 2))
    cache_chunk(gb(far), gb(theirs(nz // 2)))

    def finish(t, _):
        here = pl.ds(pl.multiple_of(t * group, group), group)
        done = [(acc[r * tiles + t] / tot[r * tiles + t]).T.reshape(group, heads, size) for r in range(2)]
        i = logical(me, t * group + lax.broadcasted_iota(jnp.int32, (group, heads, size), 0))
        for r in range(2):
            value = jnp.where(swap, done[1 - r], done[r])
            out[r, here] = jnp.where(i < nlen[r], value, 0.0).astype(out.dtype)
        return 0

    lax.fori_loop(0, tiles, finish, 0)
    for c in started:
        c.wait_send()


def shards(nz, queries, span_k, span_v, cache_k, cache_v, cached_len, new_len, prefill_flag, block_order):
    rows, count, heads, size = queries.shape
    n_ctx = lax.axis_size("ctx")
    smem = pl.BlockSpec(memory_space=pltpu.SMEM)
    hbm = pl.BlockSpec(memory_space=pl.ANY)
    vmem = pl.BlockSpec(memory_space=pltpu.VMEM)
    tiles = count * heads // TILE
    keys = 4 * count
    bf16, f32, dma = jnp.bfloat16, jnp.float32, pltpu.SemaphoreType.DMA
    inputs = [queries] + [a[:, :, 0] for a in (span_k, span_v, cache_k, cache_v)]
    return pl.pallas_call(
        functools.partial(main_kernel, nz),
        out_shape=jax.ShapeDtypeStruct(queries.shape, queries.dtype),
        in_specs=[smem] * 4 + [hbm] * 5,
        out_specs=vmem,
        scratch_shapes=[pltpu.VMEM(a.shape, bf16) for a in inputs]
        + [
            pltpu.VMEM((rows, count, size), f32),
            pltpu.VMEM((rows, count, size), f32),
            pltpu.VMEM((n_ctx, 4, count, size), bf16),
            pltpu.VMEM((n_ctx, 4, count, size), bf16),
            pltpu.VMEM((2 * tiles, 2 * size, TILE), bf16),
            pltpu.VMEM((2, keys, 2 * size), bf16),
            pltpu.VMEM((2, size, keys), bf16),
            [pltpu.VMEM((keys, TILE), f32)] * tiles,
            [pltpu.VMEM((1, TILE), f32)] * tiles,
            pltpu.VMEM((2 * tiles, size, TILE), f32),
            pltpu.VMEM((2 * tiles, 1, TILE), f32),
            pltpu.VMEM((2 * tiles, 1, TILE), f32),
            dma((5,)),
            dma((2 * n_ctx,)),
            dma((n_ctx,)),
            dma((2 * n_ctx,)),
            dma((n_ctx,)),
            dma((2,)),
            dma((2,)),
        ],
        compiler_params=pltpu.CompilerParams(collective_id=0, has_side_effects=True, vmem_limit_bytes=67043328),
        name="gather_attend",
    )(prefill_flag, cached_len, new_len, block_order, *inputs)


def solution(mesh):
    nz = mesh.shape["ctx"] // 2
    four = P("batch", "ctx", "tp", None)
    return jax.shard_map(
        functools.partial(shards, nz),
        mesh=mesh,
        in_specs=(four,) * 5 + (P("batch"),) * 3 + (P(),),
        out_specs=four,
        check_vma=False,
    )
```

time: 70.1 us -> 50.1 us (0.71)
  Pallas kernels: 63.4 us -> 47.6 us
  other arithmetic: 3.01 us -> 0 us
  local copies, waits for them, and re-layouts: 3.52 us -> 2.38 us
    pallas_call x1, Pallas kernels: 61.3 us -> 47.6 us  [shards(): pl.pallas_call(functools.partial(main_kernel, nz), out_shape=jax.ShapeDty...]
    pallas_call x1 -> x0, Pallas kernels: 2.04 us -> none  [shards(): pl.pallas_call(prep_kernel, out_shape=(packed, packed), in_specs=[smem] +...]
    unnamed x19 -> x1, local copies, waits for them, and re-layouts: 3.43 us -> 2.38 us
    concatenate x1 -> x0, other arithmetic: 0.82 us -> none  [trig_tables(): jnp.concatenate([cosine, cosine], -1)]
    mul x1 -> x0, other arithmetic: 0.82 us -> none  [shards(): lax.dynamic_slice(block_order, (2 * me,), (2,))[:, None] * blk]
where the time goes in v2:
time: 50.1 us; the launch traced here: 50 us
  Pallas kernels  47.6 us (95%)
  local copies, waits for them, and re-layouts  2.38 us (5%)
    pallas_call x1, Pallas kernels, shards(): pl.pallas_call(functools.partial(main_kernel, nz), out_shape=jax.ShapeDty...  47.6 us
    unnamed x1, local copies, waits for them, and re-layouts  2.38 us

profile of v2, /device:TPU:16, one launch (start us, length us, event | category | flops | bytes accessed | tf_op | source)
XLA Modules:
  0.0 50.0 jit_solution(15831503790707261796)
XLA Ops:
  0.0 47.6 %gather_attend.1 = bf16[2,128,16,128]{3,2,1,0:T(8,128)(2,1)} custom-call(s32[2]{0:T(128)} %flag.1, s32[2]{0:T(128)} %clen.1, s32[2]{0:T(128)} %nlen.1, s32[32]{0:T(128)} %order.1, bf16[2,128,16,128]{3,2,1,0:T(8,128)(2,1)} %q_hbm.1, bf16[2,128,128]{2,1,0:T(8,128)(2,1)} %bitcast.6, bf16[2,128,128]{2,1,0:T(8,128)(2,1)} %bitcast.7, ...), custom_call_target="tpu_custom_call" | custom-call | tf_op jit(solution)/shard_map/gather_attend/pallas_call | solution.py:307
  47.6 2.4 %copy.11 = bf16[2,128,16,128]{3,2,1,0:T(8,128)(2,1)} copy(bf16[2,128,16,128]{3,2,1,0:T(8,128)(2,1)} %gather_attend.1) | data formatting | bytes 2097152

commit v3 on v2

--- a/solution.py
+++ b/solution.py
@@ -142,6 +142,7 @@
     send_g(me, other)
 
     loads[4].wait()
+    vx[:, size:] = jnp.ones((2, 16, vx.shape[2]), jnp.bfloat16)
 
     def prepare(t, _):
         here = pl.ds(pl.multiple_of(t * group, group), group)
@@ -165,28 +166,29 @@
     def bias(visible):
         return jnp.where(visible, 0.0, NEG).astype(jnp.bfloat16)
 
-    def scores(t, at, row):
-        s = jnp.dot(kx[row], qt[at], preferred_element_type=jnp.float32)
-        s_tiles[t][...] = s
+    def scores(t, at, row, keys):
+        s = jnp.dot(kx[row, 0:keys], qt[at], preferred_element_type=jnp.float32)
+        s_tiles[t][0:keys] = s
         m_tiles[t][...] = jnp.max(s, axis=0, keepdims=True)
 
-    def absorb(t, at, row):
+    def absorb(t, at, row, keys):
         old = top[at]
         new = jnp.maximum(old, m_tiles[t][...])
-        p = jnp.exp2((s_tiles[t][...] - new) * scale)
+        p = jnp.exp2((s_tiles[t][0:keys] - new) * scale)
         fade = jnp.exp2((old - new) * scale)
-        tot[at] = tot[at] * fade + jnp.sum(p, axis=0, keepdims=True)
-        acc[at] = acc[at] * fade + jnp.dot(vx[row], p.astype(jnp.bfloat16), preferred_element_type=jnp.float32)
+        both = jnp.dot(vx[row, :, 0:keys], p.astype(jnp.bfloat16), preferred_element_type=jnp.float32)
+        acc[at] = acc[at] * fade + both[0:size]
+        tot[at] = tot[at] * fade + both[size : size + 1]
         top[at] = new
 
-    def compute(row):
-        ahead = 2
+    def compute(row, keys):
+        ahead = 4
         for t in range(ahead):
-            scores(t, row * tiles + t, row)
+            scores(t, row * tiles + t, row, keys)
         for t in range(tiles):
             if t + ahead < tiles:
-                scores(t + ahead, row * tiles + t + ahead, row)
-            absorb(t, row * tiles + t, row)
+                scores(t + ahead, row * tiles + t + ahead, row, keys)
+            absorb(t, row * tiles + t, row, keys)
 
     def cache_chunk(*blocks):
         for j, (ref, slot) in enumerate(blocks):
@@ -194,8 +196,8 @@
                 at = (2 * j + h) * piece
                 kx[0, at : at + piece, 0:size] = ref[h]
                 kx[0, at : at + piece, size : 2 * size] = bias(slot * 2 * piece + h * piece + line < cached)
-                vx[0, :, at : at + piece] = ref[2 + h]
-        compute(0)
+                vx[0, 0:size, at : at + piece] = ref[2 + h]
+        compute(0, 2 * piece * len(blocks))
 
     def span_chunk(*blocks):
         for j, (ref, slot) in enumerate(blocks):
@@ -204,10 +206,10 @@
             for r in range(2):
                 kx[r, at : at + piece, 0:size] = ref[r]
                 kx[r, at : at + piece, size : 2 * size] = bias((k_index <= q_index) & (k_index < live[r]))
-                vx[r, :, at : at + piece] = ref[2 + r]
+                vx[r, 0:size, at : at + piece] = ref[2 + r]
 
         def one(r, _):
-            compute(r)
+            compute(r, piece * len(blocks))
             return 0
 
         lax.fori_loop(0, 2, one, 0)
@@ -267,6 +269,7 @@
     got_f(theirs(3))
     got_f(theirs(-3))
     send_f(theirs(3), down)
+    span_chunk(fb(theirs(3)), fb(theirs(-3)))
     far = mine(nz // 2)
     for part in range(2):
         got(gbuf.at[far, pl.ds(2 * part, 2)], gz_recv.at[part])
@@ -274,11 +277,12 @@
     got_g(theirs(3))
     got_g(theirs(-3))
     cache_chunk(gb(theirs(3)), gb(theirs(-3)))
+    cache_chunk(gb(far))
     got_f(far)
     got_f(theirs(nz // 2))
-    span_chunk(fb(theirs(3)), fb(theirs(-3)), fb(far), fb(theirs(nz // 2)))
+    span_chunk(fb(far), fb(theirs(nz // 2)))
     got_g(theirs(nz // 2))
-    cache_chunk(gb(far), gb(theirs(nz // 2)))
+    cache_chunk(gb(theirs(nz // 2)))
 
     def finish(t, _):
         here = pl.ds(pl.multiple_of(t * group, group), group)
@@ -304,6 +308,8 @@
     keys = 4 * count
     bf16, f32, dma = jnp.bfloat16, jnp.float32, pltpu.SemaphoreType.DMA
     inputs = [queries] + [a[:, :, 0] for a in (span_k, span_v, cache_k, cache_v)]
+    placed = [pltpu.with_memory_space_constraint(a, pltpu.HBM) for a in inputs]
+    scalars = [pltpu.with_memory_space_constraint(a, pltpu.HBM) for a in (prefill_flag, cached_len, new_len, block_order)]
     return pl.pallas_call(
         functools.partial(main_kernel, nz),
         out_shape=jax.ShapeDtypeStruct(queries.shape, queries.dtype),
@@ -317,7 +323,7 @@
             pltpu.VMEM((n_ctx, 4, count, size), bf16),
             pltpu.VMEM((2 * tiles, 2 * size, TILE), bf16),
             pltpu.VMEM((2, keys, 2 * size), bf16),
-            pltpu.VMEM((2, size, keys), bf16),
+            pltpu.VMEM((2, size + 16, keys), bf16),
             [pltpu.VMEM((keys, TILE), f32)] * tiles,
             [pltpu.VMEM((1, TILE), f32)] * tiles,
             pltpu.VMEM((2 * tiles, size, TILE), f32),
@@ -331,9 +337,9 @@
             dma((2,)),
             dma((2,)),
         ],
-        compiler_params=pltpu.CompilerParams(collective_id=0, has_side_effects=True, vmem_limit_bytes=67043328),
+        compiler_params=pltpu.CompilerParams(collective_id=0, has_side_effects=True, vmem_limit_bytes=51 * 1024 * 1024),
         name="gather_attend",
-    )(prefill_flag, cached_len, new_len, block_order, *inputs)
+    )(*scalars, *placed)
 
 
 def solution(mesh):

time: 50.1 us -> 45.2 us (0.902)
  Pallas kernels: 47.6 us -> 44.1 us
  local copies, waits for them, and re-layouts: 2.38 us -> 0.97 us
    pallas_call x1, Pallas kernels: 47.6 us -> 44.1 us  [shards(): pl.pallas_call(functools.partial(main_kernel, nz), out_shape=jax.ShapeDty...]
    unnamed x1, local copies, waits for them, and re-layouts: 2.38 us -> 0.97 us
where the time goes in v3:
time: 45.2 us; the launch traced here: 45.1 us
  Pallas kernels  44.1 us (98%)
  local copies, waits for them, and re-layouts  0.97 us (2%)
    pallas_call x1, Pallas kernels, shards(): pl.pallas_call(functools.partial(main_kernel, nz), out_shape=jax.ShapeDty...  44.1 us
    unnamed x1, local copies, waits for them, and re-layouts  0.97 us

profile of v3, /device:TPU:16, one launch (start us, length us, event | category | flops | bytes accessed | tf_op | source)
XLA Modules:
  0.0 45.1 jit_solution(14594395438753172159)
XLA Ops:
  0.0 44.1 %gather_attend.1 = bf16[2,128,16,128]{3,2,1,0:T(8,128)(2,1)S(1)} custom-call(s32[2]{0:T(128)} %flag.1, s32[2]{0:T(128)} %clen.1, s32[2]{0:T(128)} %nlen.1, s32[32]{0:T(128)} %order.1, bf16[2,128,16,128]{3,2,1,0:T(8,128)(2,1)} %q_hbm.1, bf16[2,128,128]{2,1,0:T(8,128)(2,1)} %bitcast.6, bf16[2,128,128]{2,1,0:T(8,128)(2,1)} %bitcast.7, ...), custom_call_target="tpu_custom_call" | custom-call | tf_op jit(solution)/shard_map/gather_attend/pallas_call | solution.py:313
  44.1 1.0 %copy.11 = bf16[2,128,16,128]{3,2,1,0:T(8,128)(2,1)} copy(bf16[2,128,16,128]{3,2,1,0:T(8,128)(2,1)S(1)} %gather_attend.1) | data formatting | bytes 2097152

commit v4 on v3

--- a/solution.py
+++ b/solution.py
@@ -36,7 +36,7 @@
 def main_kernel(
     nz, flag, clen, nlen, order, q_hbm, sk_hbm, sv_hbm, ck_hbm, cv_hbm, out,
     q, sk, sv, ck, cv, cos, sin, fbuf, gbuf, qt, kx, vx, s_tiles, m_tiles, acc, top, tot,
-    in_sem, f_send, f_recv, g_send, g_recv, gz_send, gz_recv,
+    in_sem, f_send, f_recv, g_send, g_recv, h_send, h_recv,
 ):
     loads = [
         pltpu.make_async_copy(src, dst, in_sem.at[i])
@@ -100,9 +100,9 @@
 
     pl.semaphore_wait(barrier, 3)
     started = []
-    counts = {"f": 0, "g": 0, "z": 0}
-    sends = {"f": f_send, "g": g_send, "z": gz_send}
-    recvs = {"f": f_recv, "g": g_recv, "z": gz_recv}
+    counts = {"f": 0, "g": 0, "h": 0}
+    sends = {"f": f_send, "g": g_send, "h": h_send}
+    recvs = {"f": f_recv, "g": g_recv, "h": h_recv}
 
     def send(kind, src, dst, slot, peer):
         c = pltpu.make_async_remote_copy(
@@ -119,9 +119,11 @@
     def send_g(slot, peer):
         send("g", gbuf.at[slot], gbuf.at[slot], slot, peer)
 
+    def half_of(slot, part):
+        return fbuf.at[slot, pl.ds(2 * part, 2)]
+
     def send_half(slot, part, peer):
-        ref = gbuf.at[slot, pl.ds(2 * part, 2)]
-        send("z", ref, ref, part, peer)
+        send("h", half_of(slot, part), half_of(slot, part), part, peer)
 
     def got(buf, sem):
         pltpu.make_async_remote_copy(
@@ -130,6 +132,9 @@
 
     def got_f(slot):
         got(fbuf.at[slot], f_recv.at[slot])
+
+    def got_half(slot, part):
+        got(half_of(slot, part), h_recv.at[part])
 
     def got_g(slot):
         got(gbuf.at[slot], g_recv.at[slot])
@@ -141,8 +146,9 @@
     send_f(me, down)
     send_g(me, other)
 
+    vx[:, size:] = jnp.ones((3, 16, vx.shape[2]), jnp.bfloat16)
+
     loads[4].wait()
-    vx[:, size:] = jnp.ones((2, 16, vx.shape[2]), jnp.bfloat16)
 
     def prepare(t, _):
         here = pl.ds(pl.multiple_of(t * group, group), group)
@@ -166,40 +172,43 @@
     def bias(visible):
         return jnp.where(visible, 0.0, NEG).astype(jnp.bfloat16)
 
-    def scores(t, at, row, keys):
-        s = jnp.dot(kx[row, 0:keys], qt[at], preferred_element_type=jnp.float32)
+    def scores(t, at, buf, keys):
+        s = jnp.dot(kx[buf, 0:keys], qt[at], preferred_element_type=jnp.float32)
         s_tiles[t][0:keys] = s
         m_tiles[t][...] = jnp.max(s, axis=0, keepdims=True)
 
-    def absorb(t, at, row, keys):
+    def absorb(t, at, buf, keys):
         old = top[at]
         new = jnp.maximum(old, m_tiles[t][...])
         p = jnp.exp2((s_tiles[t][0:keys] - new) * scale)
         fade = jnp.exp2((old - new) * scale)
-        both = jnp.dot(vx[row, :, 0:keys], p.astype(jnp.bfloat16), preferred_element_type=jnp.float32)
+        both = jnp.dot(vx[buf, :, 0:keys], p.astype(jnp.bfloat16), preferred_element_type=jnp.float32)
         acc[at] = acc[at] * fade + both[0:size]
         tot[at] = tot[at] * fade + both[size : size + 1]
         top[at] = new
 
-    def compute(row, keys):
-        ahead = 4
+    def compute(row, keys, buf):
+        ahead = 4 if keys > TILE else tiles
         for t in range(ahead):
-            scores(t, row * tiles + t, row, keys)
+            scores(t, row * tiles + t, buf, keys)
         for t in range(tiles):
             if t + ahead < tiles:
-                scores(t + ahead, row * tiles + t + ahead, row, keys)
-            absorb(t, row * tiles + t, row, keys)
-
-    def cache_chunk(*blocks):
+                scores(t + ahead, row * tiles + t + ahead, buf, keys)
+            absorb(t, row * tiles + t, buf, keys)
+
+    def cache_operands(*blocks):
         for j, (ref, slot) in enumerate(blocks):
             for h in range(2):
                 at = (2 * j + h) * piece
-                kx[0, at : at + piece, 0:size] = ref[h]
-                kx[0, at : at + piece, size : 2 * size] = bias(slot * 2 * piece + h * piece + line < cached)
-                vx[0, 0:size, at : at + piece] = ref[2 + h]
-        compute(0, 2 * piece * len(blocks))
-
-    def span_chunk(*blocks):
+                kx[2, at : at + piece, 0:size] = ref[h]
+                kx[2, at : at + piece, size : 2 * size] = bias(slot * 2 * piece + h * piece + line < cached)
+                vx[2, 0:size, at : at + piece] = ref[2 + h]
+
+    def cache_chunk(*blocks):
+        cache_operands(*blocks)
+        compute(0, 2 * piece * len(blocks), 2)
+
+    def span_operands(*blocks):
         for j, (ref, slot) in enumerate(blocks):
             at = j * piece
             k_index = logical(slot, line)
@@ -208,8 +217,11 @@
                 kx[r, at : at + piece, size : 2 * size] = bias((k_index <= q_index) & (k_index < live[r]))
                 vx[r, 0:size, at : at + piece] = ref[2 + r]
 
+    def span_chunk(*blocks):
+        span_operands(*blocks)
+
         def one(r, _):
-            compute(r, piece * len(blocks))
+            compute(r, piece * len(blocks), r)
             return 0
 
         lax.fori_loop(0, 2, one, 0)
@@ -225,64 +237,73 @@
     def on(d):
         return down if d > 0 else up
 
-    def pass_f(*slots):
-        for slot, d in slots:
-            got_f(slot)
-            send_f(slot, on(d))
-
-    def pass_g(*distances):
-        for d in distances:
-            got_g(mine(d))
-            send_g(mine(d), on(d))
-            send_g(mine(d), other)
-
     got_f(other)
+    send_f(other, down)
     send_f(other, up)
-    send_f(other, down)
-    pass_g(1, -1)
+    for d in (1, -1):
+        got_g(mine(d))
+        send_g(mine(d), on(d))
+        send_g(mine(d), other)
     cache_chunk(gb(mine(1)), gb(mine(-1)))
-    pass_f((mine(1), 1), (mine(-1), -1))
+    for d in (1, -1):
+        got_f(mine(d))
+        send_f(mine(d), on(d))
     got_g(other)
     cache_chunk(gb(me), gb(other))
     span_chunk(fb(me), fb(other), fb(mine(1)), fb(mine(-1)))
-    pass_f((theirs(1), 1), (theirs(-1), -1))
-    pass_g(2, -2)
+    for d in (1, -1):
+        got_f(theirs(d))
+        send_f(theirs(d), on(d))
+    for d in (2, -2):
+        got_g(mine(d))
+        send_g(mine(d), on(d))
+        send_g(mine(d), other)
+    cache_chunk(gb(mine(2)), gb(mine(-2)))
+    for d in (2, -2):
+        got_f(mine(d))
+        send_f(mine(d), on(d))
+    span_chunk(fb(theirs(1)), fb(theirs(-1)), fb(mine(2)), fb(mine(-2)))
     got_g(theirs(1))
     got_g(theirs(-1))
     cache_chunk(gb(theirs(1)), gb(theirs(-1)))
-    cache_chunk(gb(mine(2)), gb(mine(-2)))
-    pass_f((mine(2), 2), (mine(-2), -2))
-    span_chunk(fb(theirs(1)), fb(theirs(-1)), fb(mine(2)), fb(mine(-2)))
-    pass_f((theirs(2), 2), (theirs(-2), -2))
-    for d in (3, -3):
-        got_g(mine(d))
-        send_half(mine(d), 0 if d < 0 else 1, on(d))
-        send_g(mine(d), other)
+    got_f(theirs(2))
+    send_f(theirs(2), down)
+    got_g(mine(-3))
+    send_g(mine(-3), up)
+    got_g(mine(3))
+    send_g(mine(3), other)
+    send_g(mine(-3), other)
+    got_f(theirs(-2))
+    send_f(theirs(-2), up)
+    cache_chunk(gb(mine(3)), gb(mine(-3)))
     got_g(theirs(2))
     got_g(theirs(-2))
     cache_chunk(gb(theirs(2)), gb(theirs(-2)))
-    cache_chunk(gb(mine(3)), gb(mine(-3)))
     got_f(mine(3))
+    send_half(mine(3), 1, down)
     got_f(mine(-3))
-    send_f(mine(-3), up)
+    send_half(mine(-3), 0, up)
     span_chunk(fb(theirs(2)), fb(theirs(-2)), fb(mine(3)), fb(mine(-3)))
+    far, far_other = mine(nz // 2), theirs(nz // 2)
     got_f(theirs(3))
-    got_f(theirs(-3))
     send_f(theirs(3), down)
-    span_chunk(fb(theirs(3)), fb(theirs(-3)))
-    far = mine(nz // 2)
-    for part in range(2):
-        got(gbuf.at[far, pl.ds(2 * part, 2)], gz_recv.at[part])
+    got_g(far)
     send_g(far, other)
     got_g(theirs(3))
+    cache_chunk(gb(far), gb(theirs(3)))
     got_g(theirs(-3))
-    cache_chunk(gb(theirs(3)), gb(theirs(-3)))
-    cache_chunk(gb(far))
-    got_f(far)
-    got_f(theirs(nz // 2))
-    span_chunk(fb(far), fb(theirs(nz // 2)))
-    got_g(theirs(nz // 2))
-    cache_chunk(gb(theirs(nz // 2)))
+    cache_chunk(gb(theirs(-3)))
+    got_f(theirs(-3))
+    span_chunk(fb(theirs(3)), fb(theirs(-3)))
+    got_half(far, 0)
+    got_half(far, 1)
+    got_f(far_other)
+    got_g(far_other)
+    cache_operands(gb(far_other))
+    span_operands(fb(far), fb(far_other))
+    compute(0, 2 * piece, 2)
+    compute(1, 2 * piece, 1)
+    compute(0, 2 * piece, 0)
 
     def finish(t, _):
         here = pl.ds(pl.multiple_of(t * group, group), group)
@@ -322,8 +343,8 @@
             pltpu.VMEM((n_ctx, 4, count, size), bf16),
             pltpu.VMEM((n_ctx, 4, count, size), bf16),
             pltpu.VMEM((2 * tiles, 2 * size, TILE), bf16),
-            pltpu.VMEM((2, keys, 2 * size), bf16),
-            pltpu.VMEM((2, size + 16, keys), bf16),
+            pltpu.VMEM((3, keys, 2 * size), bf16),
+            pltpu.VMEM((3, size + 16, keys), bf16),
             [pltpu.VMEM((keys, TILE), f32)] * tiles,
             [pltpu.VMEM((1, TILE), f32)] * tiles,
             pltpu.VMEM((2 * tiles, size, TILE), f32),

time: 45.2 us -> 44.4 us (0.982)
  Pallas kernels: 44.1 us -> 43.3 us
    pallas_call x1, Pallas kernels: 44.1 us -> 43.3 us  [shards(): pl.pallas_call(functools.partial(main_kernel, nz), out_shape=jax.ShapeDty...]
where the time goes in v4:
time: 44.4 us; the launch traced here: 44.3 us
  Pallas kernels  43.3 us (98%)
  local copies, waits for them, and re-layouts  0.97 us (2%)
    pallas_call x1, Pallas kernels, shards(): pl.pallas_call(functools.partial(main_kernel, nz), out_shape=jax.ShapeDty...  43.3 us
    unnamed x1, local copies, waits for them, and re-layouts  0.97 us

profile of v4, /device:TPU:16, one launch (start us, length us, event | category | flops | bytes accessed | tf_op | source)
XLA Modules:
  0.0 44.3 jit_solution(14404118773094031397)
XLA Ops:
  0.0 43.3 %gather_attend.1 = bf16[2,128,16,128]{3,2,1,0:T(8,128)(2,1)S(1)} custom-call(s32[2]{0:T(128)} %flag.1, s32[2]{0:T(128)} %clen.1, s32[2]{0:T(128)} %nlen.1, s32[32]{0:T(128)} %order.1, bf16[2,128,16,128]{3,2,1,0:T(8,128)(2,1)} %q_hbm.1, bf16[2,128,128]{2,1,0:T(8,128)(2,1)} %bitcast.6, bf16[2,128,128]{2,1,0:T(8,128)(2,1)} %bitcast.7, ...), custom_call_target="tpu_custom_call" | custom-call | tf_op jit(solution)/shard_map/gather_attend/pallas_call | solution.py:334
  43.3 1.0 %copy.11 = bf16[2,128,16,128]{3,2,1,0:T(8,128)(2,1)} copy(bf16[2,128,16,128]{3,2,1,0:T(8,128)(2,1)S(1)} %gather_attend.1) | data formatting | bytes 2097152
